TPU v7x, 32 devices: a whole 2x2x4 slice. The times are simulated.
32 devices in a mesh: pipe: 4 (over x, core), vocab: 8 (over z, y).
Axes of the slice: x: 2, y: 2, z: 4, core: 2. Of those that a mesh axis runs over, the one named last changes fastest.
Arguments:
- hidden: bfloat16 [4, 128, 4096], P('pipe'), may hold values from -60 to 60
- norm_gain: float32 [4096], replicated, may hold values from 0.5 to 1.5
- out_weight: bfloat16 [128256, 4096], P(('pipe', 'vocab')), may hold values from -4 to 4
- targets: int32 [4, 128], P('pipe'), may hold values from 0 to 128255
- loss_mask: int32 [4, 128], P('pipe'), may hold values from 0 to 1, as said below
- slot_position: int32 [4, 128], P('pipe'), may hold values from 0 to 127, each once within a row
- counts: int32 [4], replicated, may hold values from 1 to 128, 320 in all
- loss_scale: float32 [], replicated, may hold values from 4096 to 32768
Outputs:
- loss: float32 [], replicated
- grad_hidden: bfloat16 [4, 128, 4096], P('pipe')
Inputs may be any that keep to these rules, and one draw needn't show every extreme that they name: The 4 counts sum to exactly 320, and one of them equals 128. Each row of slot_position holds every number of 0 to 127 once. Each row of loss_mask holds at least 64 ones.
All inputs are finite; a program needn't handle non-finite values.
Results may differ from a plain program's by a relative error of at most 0.0034.
Values may be sent and summed in bfloat16 or wider, within the bound.
A program may use at most 128 MiB of HBM per device.

v0:
```python
import jax
import jax.numpy as jnp
from jax import lax
from jax.sharding import PartitionSpec as P

EPSILON = 1e-05


def rms_scale(values, norm_gain):
    mean_square = jnp.mean(values * values, axis=-1, keepdims=True)
    return values * lax.rsqrt(mean_square + EPSILON) * norm_gain


def pull_rows(rows, norm_gain, cotangent):
    pullback = jax.vjp(lambda values: rms_scale(values, norm_gain), rows)[1]
    return pullback(cotangent)[0].astype(jnp.bfloat16)


def softmax_stats(logits, local_target):
    row_top = lax.pmax(jnp.max(logits, axis=1), ("pipe", "vocab"))
    local_total = jnp.sum(jnp.exp(logits - row_top[:, None]), axis=1)
    exp_total, target_logit = lax.psum((local_total, local_target), ("pipe", "vocab"))
    return (row_top + jnp.log(exp_total), target_logit)


def body(hidden, norm_gain, out_weight, targets, loss_mask, slot_position, counts, loss_scale):
    micro_slots = hidden.shape[1]
    model_width = hidden.shape[2]
    shard_words = out_weight.shape[0]
    offset = lax.axis_index(("pipe", "vocab")) * shard_words
    own_rows = hidden.reshape(micro_slots, model_width).astype(jnp.float32)
    own_normed = rms_scale(own_rows, norm_gain).astype(jnp.bfloat16)
    all_normed, all_targets, all_masks, all_positions = (
        lax.all_gather(own_normed, "pipe", axis=0, tiled=True),
        lax.all_gather(targets.reshape(micro_slots), "pipe", axis=0, tiled=True),
        lax.all_gather(loss_mask.reshape(micro_slots), "pipe", axis=0, tiled=True),
        lax.all_gather(slot_position.reshape(micro_slots), "pipe", axis=0, tiled=True),
    )
    rows_total = all_normed.shape[0]
    micro_index = jnp.arange(rows_total, dtype=jnp.int32) // micro_slots
    count_row = jnp.sum(
        jnp.where(
            micro_index[:, None] == jnp.arange(counts.shape[0], dtype=jnp.int32)[None, :],
            counts[None, :],
            0,
        ),
        axis=1,
    )
    inside = all_positions < count_row
    token_weight = jnp.where(inside & (all_masks == 1), 1.0, 0.0).astype(jnp.float32)
    weight_total = jnp.sum(token_weight)
    work_normed, work_targets, work_weight = (all_normed, all_targets, token_weight)
    logits = lax.dot_general(
        work_normed, out_weight, (((1,), (1,)), ((), ())), preferred_element_type=jnp.float32
    )
    is_target = (
        jnp.arange(shard_words, dtype=jnp.int32)[None, :] == (work_targets - offset)[:, None]
    )
    local_target = jnp.sum(jnp.where(is_target, logits, 0.0), axis=1)
    log_total, target_logit = softmax_stats(logits, local_target)
    loss = jnp.sum(work_weight * (log_total - target_logit)) / weight_total
    token_coef = loss_scale * work_weight / weight_total
    logit_grad = (
        (jnp.exp(logits - log_total[:, None]) - is_target.astype(jnp.float32)) * token_coef[:, None]
    ).astype(jnp.bfloat16)
    work_grad = jnp.dot(logit_grad, out_weight, preferred_element_type=jnp.float32)
    grad_cube = work_grad.reshape(rows_total // micro_slots, micro_slots, model_width)
    micro_grad = lax.psum_scatter(grad_cube, "pipe", scatter_dimension=0, tiled=True)
    summed = lax.psum(micro_grad, "vocab")
    grad_out = pull_rows(own_rows, norm_gain, summed.reshape(micro_slots, model_width))
    return (loss, grad_out.reshape(1, micro_slots, model_width))


def solution(mesh):
    in_specs = (
        P("pipe", None, None),
        P(),
        P(("pipe", "vocab"), None),
        P("pipe", None),
        P("pipe", None),
        P("pipe", None),
        P(),
        P(),
    )
    out_specs = (P(), P("pipe", None, None))
    return jax.shard_map(body, mesh=mesh, in_specs=in_specs, out_specs=out_specs, check_vma=False)
```

profile of v0, /device:TPU:0, one launch (start us, length us, event | category | flops | bytes accessed | tf_op | source)
XLA Modules:
  0.0 372.7 jit_solution(8846889576664135234)
XLA Ops:
  7.2 0.0 copy-start.3
  7.2 0.0 copy-start.4
  7.2 0.0 copy-start.5
  7.2 0.0 copy-start.6
  7.2 0.0 all-gather.5.cloned.1.call-start
  7.3 1.5 fusion.7
  8.8 2.5 fusion.9
  11.3 0.0 all-gather.5.cloned.1.call-update
  11.3 0.0 reduce-scatter.2.cloned.1.call-start
  12.0 0.0 copy-done.3
  12.0 6.0 %all-gather.2 = s32[1,512]{1,0:T(1,128)S(1)} all-gather(s32[1,128]{1,0:T(1,128)S(1)} %copy-done.3), channel_id=4, replica_groups=mesh['pipe'=4,'vocab'=8] {'pipe'}, dimensions={1}, use_global_device_ids=true | all-gather | bytes 2560 | tf_op jit(solution)/shard_map/all_gather | solution.py:35
  18.1 0.0 copy-done.4
  18.1 5.4 %all-gather.1 = s32[1,512]{1,0:T(1,128)S(1)} all-gather(s32[1,128]{1,0:T(1,128)S(1)} %copy-done.4), channel_id=3, replica_groups=mesh['pipe'=4,'vocab'=8] {'pipe'}, dimensions={1}, use_global_device_ids=true | all-gather | bytes 2560 | tf_op jit(solution)/shard_map/all_gather | solution.py:36
  23.4 0.0 copy-done.5
  23.4 5.2 %all-gather = s32[1,512]{1,0:T(1,128)S(1)} all-gather(s32[1,128]{1,0:T(1,128)S(1)} %copy-done.5), channel_id=2, replica_groups=mesh['pipe'=4,'vocab'=8] {'pipe'}, dimensions={1}, use_global_device_ids=true | all-gather | bytes 2560 | tf_op jit(solution)/shard_map/all_gather | solution.py:37
  28.6 0.0 copy-done.6
  28.6 0.1 select_reduce_fusion.1
  28.7 19.9 %all-gather.5.cloned.1.call-done = bf16[512,4096]{1,0:T(8,128)(2,1)} async-done(((bf16[128,4096]{1,0:T(8,128)(2,1)}), bf16[512,4096]{1,0:T(8,128)(2,1)}) %all-gather.5.cloned.1.call-update) | async-done | bytes 4194320 | tf_op jit(solution)/shard_map/all_gather | solution.py:34
  48.7 23.8 %fusion.18 = (f32[512]{0:T(512)S(1)}, f32[512,4008]{0,1:T(8,128)}) fusion(bf16[512,4096]{1,0:T(8,128)(2,1)} %all-gather.5.cloned.1.call-done, bf16[4008,4096]{1,0:T(8,128)(2,1)} %param.10), kind=kOutput, calls=%fused_computation.41 | convolution fusion | flops 16812822528 | bytes 45238272 | tf_op jit(solution)/shard_map/dot_general | solution.py:53
  72.4 39.2 %pmax.7 = f32[512]{0:T(512)S(1)} all-reduce(f32[512]{0:T(512)S(1)} %get-tuple-element.10), channel_id=1, replica_groups=mesh['pipe'=4,'vocab'=8] {'pipe','vocab'}, use_global_device_ids=true, to_apply=%region_3.4 | all-reduce | flops 512 | bytes 4096 | tf_op jit(solution)/shard_map/pmax | solution.py:20
  111.7 4.5 %select_reduce_fusion = (f32[512]{0:T(512)S(1)}, f32[512]{0:T(512)S(1)}) fusion(f32[512,4008]{0,1:T(8,128)} %get-tuple-element.11, s32[512]{0:T(512)S(1)} %bitcast.27, f32[512]{0:T(512)S(1)} %pmax.7), kind=kLoop, calls=%fused_computation.1 | loop fusion | flops 10259456 | bytes 8216576 | tf_op jit(solution)/shard_map/reduce_sum | solution.py:59
  116.2 41.0 %all-reduce = (f32[512]{0:T(512)S(1)}, f32[512]{0:T(512)S(1)}) all-reduce(f32[512]{0:T(512)S(1)} %get-tuple-element.3, f32[512]{0:T(512)S(1)} %get-tuple-element.2), channel_id=1, replica_groups=mesh['pipe'=4,'vocab'=8] {'pipe','vocab'}, use_global_device_ids=true, to_apply=%region_5.6 | all-reduce | flops 1024 | bytes 8192 | tf_op jit(solution)/shard_map/psum | solution.py:22
  157.1 0.6 select_reduce_fusion.2
  157.8 0.7 fusion.13
  158.4 25.5 %fusion = f32[512,4096]{1,0:T(8,128)} fusion(bf16[4008,4096]{1,0:T(8,128)(2,1)} %param.10, f32[512,4008]{0,1:T(8,128)} %get-tuple-element.11, f32[512]{0:T(512)S(1)} %fusion.13, f32[512]{0:T(512)S(1)} %get-tuple-element.8, s32[512]{0:T(512)S(1)} %bitcast.28), kind=kOutput, calls=%fused_computation.4 | convolution fusion | flops 16823083008 | bytes 49436672 | tf_op jit(solution)/shard_map/dot_general | solution.py:66
  183.9 0.0 copy-start
  183.9 0.0 copy-start.2
  183.9 0.0 reduce-scatter.2.cloned.1.call-update
  184.0 0.0 all-reduce.3.cloned.1.call-start
  184.0 71.2 %reduce-scatter.2.cloned.1.call-done = f32[1,128,4096]{2,1,0:T(8,128)} async-done(((f32[4,128,4096]{2,1,0:T(8,128)}), f32[1,128,4096]{2,1,0:T(8,128)}) %reduce-scatter.2.cloned.1.call-update) | async-done | bytes 2097168 | tf_op jit(solution)/shard_map/reduce_scatter | solution.py:68
  255.3 0.0 all-reduce.3.cloned.1.call-update
  256.6 104.7 %all-reduce.3.cloned.1.call-done = f32[1,128,4096]{2,1,0:T(8,128)} async-done(((f32[1,128,4096]{2,1,0:T(8,128)}), f32[1,128,4096]{2,1,0:T(8,128)}) %all-reduce.3.cloned.1.call-update) | async-done | bytes 2097168 | tf_op jit(solution)/shard_map/psum | solution.py:69
  361.3 0.0 copy-done
  361.3 0.0 copy-done.2
  361.3 0.0 copy-start.1
  361.3 2.1 fusion.10
  363.4 0.1 copy-done.1
  363.5 1.5 fusion.11
  (5 shorter events, 0.0 us)
Async XLA Ops:
  7.2 4.9 %copy-start.3 = (s32[1,128]{1,0:T(1,128)S(1)}, s32[1,128]{1,0:T(1,128)}, u32[]{:S(2)}) copy-start(s32[1,128]{1,0:T(1,128)} %param.11) | copy-start | bytes 1540
  7.2 10.9 %copy-start.4 = (s32[1,128]{1,0:T(1,128)S(1)}, s32[1,128]{1,0:T(1,128)}, u32[]{:S(2)}) copy-start(s32[1,128]{1,0:T(1,128)} %param.12) | copy-start | bytes 1540
  7.2 16.2 %copy-start.5 = (s32[1,128]{1,0:T(1,128)S(1)}, s32[1,128]{1,0:T(1,128)}, u32[]{:S(2)}) copy-start(s32[1,128]{1,0:T(1,128)} %param.13) | copy-start | bytes 1540
  7.2 21.4 %copy-start.6 = (s32[4]{0:T(128)S(1)}, s32[4]{0:T(128)}, u32[]{:S(2)}) copy-start(s32[4]{0:T(128)} %param.14) | copy-start | bytes 52
  7.2 41.5 %all-gather.5.cloned.1.call-start = ((), (), s32[]{:S(2)}) async-start(), calls=%async_computation.1 | async-start | bytes 5242880 | tf_op jit(solution)/shard_map/all_gather | solution.py:34
  11.3 243.9 %reduce-scatter.2.cloned.1.call-start = ((), (), s32[]{:S(2)}) async-start(), calls=%async_computation.2 | async-start | bytes 10485760 | tf_op jit(solution)/shard_map/reduce_scatter | solution.py:68
  183.9 177.3 %copy-start = (bf16[1,128,4096]{2,1,0:T(8,128)(2,1)S(1)}, bf16[1,128,4096]{2,1,0:T(8,128)(2,1)}, u32[]{:S(2)}) copy-start(bf16[1,128,4096]{2,1,0:T(8,128)(2,1)} %param.8) | copy-start | bytes 3145732
  183.9 177.3 %copy-start.2 = (f32[4096]{0:T(1024)S(1)}, f32[4096]{0:T(1024)}, u32[]{:S(2)}) copy-start(f32[4096]{0:T(1024)} %param.9) | copy-start | bytes 49156
  184.0 177.3 %all-reduce.3.cloned.1.call-start = ((), (), s32[]{:S(2)}) async-start(), calls=%async_computation.3 | async-start | bytes 4194304 | tf_op jit(solution)/shard_map/psum | solution.py:69
  361.3 2.2 copy-start.1
Sparse Core Ops, SparseCore 0:
  11.5 37.1 all-gather.4
  184.1 71.1 reduce-scatter.1
  258.9 102.3 all-reduce.2
where the time goes:
time: 373 us
  waiting for transfers between devices  196 us (53%)
  blocking collectives  96.8 us (26%)
  matrix products  49.3 us (13%)
  between operations  16.9 us (5%)
  other arithmetic  13.6 us (4%)
    psum x1, waiting for transfers between devices, body(): summed = lax.psum(micro_grad, 'vocab')  105 us
    reduce_scatter x1, waiting for transfers between devices, body(): lax.psum_scatter(grad_cube, 'pipe', scatter_dimension=0, tiled=True)  71.2 us
    psum x1, blocking collectives, softmax_stats(): lax.psum((local_total, local_target), ('pipe', 'vocab'))  41 us
    pmax x1, blocking collectives, softmax_stats(): row_top = lax.pmax(jnp.max(logits, axis=1), ('pipe', 'vocab'))  39.2 us
    dot_general x1, matrix products, body(): jnp.dot(logit_grad, out_weight, preferred_element_type=jnp.float32)  25.5 us
    dot_general x1, matrix products, body(): lax.dot_general(work_normed, out_weight, (((1,), (1,)), ((), ())), prefer...  23.8 us
    all_gather x1, waiting for transfers between devices, body(): lax.all_gather(own_normed, 'pipe', axis=0, tiled=True)  19.9 us
  transfers between devices with their start and end apart: 3, of which 3 were waited for; matrix products, arithmetic and copies ran while one was open for 0% of the time, Pallas kernels for 0%

commit v1 on v0

--- a/solution.py
+++ b/solution.py
@@ -66,7 +66,9 @@
     work_grad = jnp.dot(logit_grad, out_weight, preferred_element_type=jnp.float32)
     grad_cube = work_grad.reshape(rows_total // micro_slots, micro_slots, model_width)
     micro_grad = lax.psum_scatter(grad_cube, "pipe", scatter_dimension=0, tiled=True)
-    summed = lax.psum(micro_grad, "vocab")
+    summed = micro_grad
+    for hop in (1, 2, 4):
+        summed = summed + lax.ppermute(summed, "vocab", [(dev, dev ^ hop) for dev in range(8)])
     grad_out = pull_rows(own_rows, norm_gain, summed.reshape(micro_slots, model_width))
     return (loss, grad_out.reshape(1, micro_slots, model_width))
 

time: 373 us -> 457 us (1.23)
  waiting for transfers between devices: 196 us -> 270 us
  starting transfers between devices: 0.12 us -> 5.62 us
    ppermute x0 -> x3, waiting for transfers between devices: none -> 178 us  [body(): lax.ppermute(summed, 'vocab', [(dev, dev ^ hop) for dev in range(8)])]
    psum x1 -> x0, waiting for transfers between devices: 105 us -> none  [body(): summed = lax.psum(micro_grad, 'vocab')]
    ppermute x0 -> x3, starting transfers between devices: none -> 5.54 us  [body(): lax.ppermute(summed, 'vocab', [(dev, dev ^ hop) for dev in range(8)])]
  transfers between devices with their start and end apart: 3 -> 5, of which waited for: 3 -> 5; matrix products, arithmetic and copies ran while one was open for 0% -> 0% of each run, Pallas kernels for 0% -> 0%
where the time goes in v1:
time: 457 us; the launch traced here: 456 us
  waiting for transfers between devices  270 us (59%)
  blocking collectives  96.9 us (21%)
  matrix products  49.3 us (11%)
  other arithmetic  17.4 us (4%)
  between operations  17.3 us (4%)
  starting transfers between devices  5.62 us (1%)
    ppermute x3, waiting for transfers between devices, body(): lax.ppermute(summed, 'vocab', [(dev, dev ^ hop) for dev in range(8)])  178 us
    reduce_scatter x1, waiting for transfers between devices, body(): lax.psum_scatter(grad_cube, 'pipe', scatter_dimension=0, tiled=True)  71.4 us
    psum x1, blocking collectives, softmax_stats(): lax.psum((local_total, local_target), ('pipe', 'vocab'))  41.1 us
    pmax x1, blocking collectives, softmax_stats(): row_top = lax.pmax(jnp.max(logits, axis=1), ('pipe', 'vocab'))  39.2 us
    dot_general x1, matrix products, body(): jnp.dot(logit_grad, out_weight, preferred_element_type=jnp.float32)  25.5 us
    dot_general x1, matrix products, body(): lax.dot_general(work_normed, out_weight, (((1,), (1,)), ((), ())), prefer...  23.7 us
    all_gather x1, waiting for transfers between devices, body(): lax.all_gather(own_normed, 'pipe', axis=0, tiled=True)  19.9 us
  transfers between devices with their start and end apart: 5, of which 5 were waited for; matrix products, arithmetic and copies ran while one was open for 0% of the time, Pallas kernels for 0%

profile of v1, /device:TPU:0, one launch (start us, length us, event | category | flops | bytes accessed | tf_op | source)
XLA Modules:
  0.0 456.2 jit_solution(1102869830318089280)
XLA Ops:
  7.2 0.0 copy-start.2
  7.2 0.0 copy-start.3
  7.2 0.0 copy-start.4
  7.2 0.0 copy-start.5
  7.2 0.0 all-gather.5.cloned.1.call-start
  7.3 1.5 fusion.7
  8.8 2.5 fusion.9
  11.3 0.0 all-gather.5.cloned.1.call-update
  11.3 0.0 reduce-scatter.2.cloned.1.call-start
  12.0 0.0 copy-done.2
  12.0 6.0 %all-gather.2 = s32[1,512]{1,0:T(1,128)S(1)} all-gather(s32[1,128]{1,0:T(1,128)S(1)} %copy-done.2), channel_id=4, replica_groups=mesh['pipe'=4,'vocab'=8] {'pipe'}, dimensions={1}, use_global_device_ids=true | all-gather | bytes 2560 | tf_op jit(solution)/shard_map/all_gather | solution.py:35
  18.1 0.0 copy-done.3
  18.1 5.4 %all-gather.1 = s32[1,512]{1,0:T(1,128)S(1)} all-gather(s32[1,128]{1,0:T(1,128)S(1)} %copy-done.3), channel_id=3, replica_groups=mesh['pipe'=4,'vocab'=8] {'pipe'}, dimensions={1}, use_global_device_ids=true | all-gather | bytes 2560 | tf_op jit(solution)/shard_map/all_gather | solution.py:36
  23.4 0.0 copy-done.4
  23.4 5.2 %all-gather = s32[1,512]{1,0:T(1,128)S(1)} all-gather(s32[1,128]{1,0:T(1,128)S(1)} %copy-done.4), channel_id=2, replica_groups=mesh['pipe'=4,'vocab'=8] {'pipe'}, dimensions={1}, use_global_device_ids=true | all-gather | bytes 2560 | tf_op jit(solution)/shard_map/all_gather | solution.py:37
  28.6 0.0 copy-done.5
  28.6 0.1 select_reduce_fusion.1
  28.7 19.9 %all-gather.5.cloned.1.call-done = bf16[512,4096]{1,0:T(8,128)(2,1)} async-done(((bf16[128,4096]{1,0:T(8,128)(2,1)}), bf16[512,4096]{1,0:T(8,128)(2,1)}) %all-gather.5.cloned.1.call-update) | async-done | bytes 4194320 | tf_op jit(solution)/shard_map/all_gather | solution.py:34
  48.7 23.7 %fusion.18 = (f32[512]{0:T(512)S(1)}, f32[512,4008]{0,1:T(8,128)}) fusion(bf16[512,4096]{1,0:T(8,128)(2,1)} %all-gather.5.cloned.1.call-done, bf16[4008,4096]{1,0:T(8,128)(2,1)} %param.10), kind=kOutput, calls=%fused_computation.41 | convolution fusion | flops 16812822528 | bytes 45238272 | tf_op jit(solution)/shard_map/dot_general | solution.py:53
  72.4 39.2 %pmax.7 = f32[512]{0:T(512)S(1)} all-reduce(f32[512]{0:T(512)S(1)} %get-tuple-element.10), channel_id=1, replica_groups=mesh['pipe'=4,'vocab'=8] {'pipe','vocab'}, use_global_device_ids=true, to_apply=%region_3.4 | all-reduce | flops 512 | bytes 4096 | tf_op jit(solution)/shard_map/pmax | solution.py:20
  111.7 4.5 select_reduce_fusion
  116.2 41.1 %all-reduce = (f32[512]{0:T(512)S(1)}, f32[512]{0:T(512)S(1)}) all-reduce(f32[512]{0:T(512)S(1)} %get-tuple-element.3, f32[512]{0:T(512)S(1)} %get-tuple-element.2), channel_id=1, replica_groups=mesh['pipe'=4,'vocab'=8] {'pipe','vocab'}, use_global_device_ids=true, to_apply=%region_5.6 | all-reduce | flops 1024 | bytes 8192 | tf_op jit(solution)/shard_map/psum | solution.py:22
  157.3 0.6 select_reduce_fusion.2
  157.9 0.7 fusion.13
  158.5 25.5 %fusion = f32[512,4096]{1,0:T(8,128)} fusion(bf16[4008,4096]{1,0:T(8,128)(2,1)} %param.10, f32[512,4008]{0,1:T(8,128)} %get-tuple-element.11, f32[512]{0:T(512)S(1)} %fusion.13, f32[512]{0:T(512)S(1)} %get-tuple-element.8, s32[512]{0:T(512)S(1)} %bitcast.28), kind=kOutput, calls=%fused_computation.4 | convolution fusion | flops 16823083008 | bytes 49436672 | tf_op jit(solution)/shard_map/dot_general | solution.py:66
  184.1 0.0 reduce-scatter.2.cloned.1.call-update
  184.1 71.4 %reduce-scatter.2.cloned.1.call-done = f32[1,128,4096]{2,1,0:T(8,128)} async-done(((f32[4,128,4096]{2,1,0:T(8,128)}), f32[1,128,4096]{2,1,0:T(8,128)}) %reduce-scatter.2.cloned.1.call-update) | async-done | bytes 2097168 | tf_op jit(solution)/shard_map/reduce_scatter | solution.py:68
  255.5 1.5 collective-permute-start
  256.9 45.9 %collective-permute-done = f32[1,128,4096]{2,1,0:T(8,128)S(1)} collective-permute-done((f32[1,128,4096]{2,1,0:T(8,128)}, f32[1,128,4096]{2,1,0:T(8,128)S(1)}, u32[]{:S(2)}, u32[]{:S(2)}) %collective-permute-start) | collective-permute-done | bytes 2097184 | tf_op jit(solution)/shard_map/ppermute | solution.py:71
  302.9 1.8 add.40
  304.7 0.0 copy-start
  304.7 0.0 copy-start.1
  304.7 1.5 collective-permute-start.1
  306.3 44.9 %collective-permute-done.1 = f32[1,128,4096]{2,1,0:T(8,128)S(1)} collective-permute-done((f32[1,128,4096]{2,1,0:T(8,128)S(1)}, f32[1,128,4096]{2,1,0:T(8,128)S(1)}, u32[]{:S(2)}, u32[]{:S(2)}) %collective-permute-start.1) | collective-permute-done | bytes 2097184 | tf_op jit(solution)/shard_map/ppermute | solution.py:71
  351.1 0.2 add.41
  351.4 2.5 collective-permute-start.2
  355.2 87.6 %collective-permute-done.2 = f32[1,128,4096]{2,1,0:T(8,128)} collective-permute-done((f32[1,128,4096]{2,1,0:T(8,128)S(1)}, f32[1,128,4096]{2,1,0:T(8,128)}, u32[]{:S(2)}, u32[]{:S(2)}) %collective-permute-start.2) | collective-permute-done | bytes 2097184 | tf_op jit(solution)/shard_map/ppermute | solution.py:71
  442.9 0.0 copy-done
  442.9 0.0 copy-done.1
  442.9 2.1 fusion.10
  445.0 3.3 fusion.11
  (5 shorter events, 0.0 us)
Async XLA Ops:
  7.2 4.9 %copy-start.2 = (s32[1,128]{1,0:T(1,128)S(1)}, s32[1,128]{1,0:T(1,128)}, u32[]{:S(2)}) copy-start(s32[1,128]{1,0:T(1,128)} %param.11) | copy-start | bytes 1540
  7.2 10.9 %copy-start.3 = (s32[1,128]{1,0:T(1,128)S(1)}, s32[1,128]{1,0:T(1,128)}, u32[]{:S(2)}) copy-start(s32[1,128]{1,0:T(1,128)} %param.12) | copy-start | bytes 1540
  7.2 16.2 %copy-start.4 = (s32[1,128]{1,0:T(1,128)S(1)}, s32[1,128]{1,0:T(1,128)}, u32[]{:S(2)}) copy-start(s32[1,128]{1,0:T(1,128)} %param.13) | copy-start | bytes 1540
  7.2 21.4 %copy-start.5 = (s32[4]{0:T(128)S(1)}, s32[4]{0:T(128)}, u32[]{:S(2)}) copy-start(s32[4]{0:T(128)} %param.14) | copy-start | bytes 52
  7.2 41.5 %all-gather.5.cloned.1.call-start = ((), (), s32[]{:S(2)}) async-start(), calls=%async_computation.1 | async-start | bytes 5242880 | tf_op jit(solution)/shard_map/all_gather | solution.py:34
  11.3 244.1 %reduce-scatter.2.cloned.1.call-start = ((), (), s32[]{:S(2)}) async-start(), calls=%async_computation.2 | async-start | bytes 10485760 | tf_op jit(solution)/shard_map/reduce_scatter | solution.py:68
  255.5 47.4 %collective-permute-start = (f32[1,128,4096]{2,1,0:T(8,128)}, f32[1,128,4096]{2,1,0:T(8,128)S(1)}, u32[]{:S(2)}, u32[]{:S(2)}) collective-permute-start(f32[1,128,4096]{2,1,0:T(8,128)} %reduce-scatter.2.cloned.1.call-done), channel_id=1, source_target_pairs={{0,1},{1,0},{2,3},{3,2},{4,5},{5,4},{6,7},{7,6},{8,9},{9,8},{10,11... | collective-permute-start | bytes 6291464 | tf_op jit(solution)/shard_map/ppermute | solution.py:71
  304.7 138.2 %copy-start = (bf16[1,128,4096]{2,1,0:T(8,128)(2,1)S(1)}, bf16[1,128,4096]{2,1,0:T(8,128)(2,1)}, u32[]{:S(2)}) copy-start(bf16[1,128,4096]{2,1,0:T(8,128)(2,1)} %param.8) | copy-start | bytes 3145732
  304.7 138.2 %copy-start.1 = (f32[4096]{0:T(1024)S(1)}, f32[4096]{0:T(1024)}, u32[]{:S(2)}) copy-start(f32[4096]{0:T(1024)} %param.9) | copy-start | bytes 49156
  304.7 46.4 %collective-permute-start.1 = (f32[1,128,4096]{2,1,0:T(8,128)S(1)}, f32[1,128,4096]{2,1,0:T(8,128)S(1)}, u32[]{:S(2)}, u32[]{:S(2)}) collective-permute-start(f32[1,128,4096]{2,1,0:T(8,128)S(1)} %add.40), channel_id=1, source_target_pairs={{0,2},{1,3},{2,0},{3,1},{4,6},{5,7},{6,4},{7,5},{8,10},{9,11},{10,... | collective-permute-start | bytes 6291464 | tf_op jit(solution)/shard_map/ppermute | solution.py:71
  351.4 91.5 %collective-permute-start.2 = (f32[1,128,4096]{2,1,0:T(8,128)S(1)}, f32[1,128,4096]{2,1,0:T(8,128)}, u32[]{:S(2)}, u32[]{:S(2)}) collective-permute-start(f32[1,128,4096]{2,1,0:T(8,128)S(1)} %add.41), channel_id=1, source_target_pairs={{0,4},{1,5},{2,6},{3,7},{4,0},{5,1},{6,2},{7,3},{8,12},{9,13},{10,... | collective-permute-start | bytes 6291464 | tf_op jit(solution)/shard_map/ppermute | solution.py:71
Sparse Core Ops, SparseCore 0:
  11.5 37.1 all-gather.4
  184.2 71.1 reduce-scatter.1
